TPU v7x, 128 devices: a whole 4x4x4 slice. The times are simulated.
128 devices in a mesh: row: 16 (over y, x), col: 8 (over z, core).
Axes of the slice: x: 4, y: 4, z: 4, core: 2. Of those that a mesh axis runs over, the one named last changes fastest.
Arguments:
- moments: float32 [2, 128, 128, 6144], P(None, None, 'row', 'col'), may hold values from -6 to 6
- owner_counts: int32 [16], replicated, may hold values from 1 to 16, 128 in all
Outputs:
- normalized: float32 [2, 32768, 6144], P(None, 'row', 'col')
- scales: float32 [2, 256], P(None, 'row')
- energy: float32 [2, 256], P(None, 'row')
Inputs may be any that keep to these rules, and one draw needn't show every extreme that they name: owner_counts sums to 128, and its largest entry is exactly 16.
All inputs are finite; a program needn't handle non-finite values.
Results may differ from a plain program's by a relative error of at most 0.00002.
Values sent between devices are 32-bit elements.
No kernel may reach another device: no remote copies, remote signals or barrier semaphores. Data moves between devices by JAX's collectives and lax.ppermute only.
A program may use at most 128 MiB of HBM per device.

v0:
```python
import jax
import jax.numpy as jnp
from jax import lax
from jax.sharding import PartitionSpec as P


def total_of_pieces(x, axis):
    return lax.all_gather(x, axis).max(0)


def sent_to_all(x, axis):
    copies = jnp.broadcast_to(x, (lax.axis_size(axis), *x.shape))
    return lax.all_to_all(copies, axis, split_axis=0, concat_axis=0, tiled=True)


def over_copies(x, axis):
    return sent_to_all(x, axis).sum(axis=0)


def on_device(moments, owner_counts):
    groups = lax.axis_size("row")
    splits = lax.axis_size("col")
    tensors, blocks_all, sub_rows, piece_width = moments.shape
    full_width = piece_width * splits
    block_rows = sub_rows * groups
    capacity = 2 * blocks_all // groups
    starts = jnp.cumsum(owner_counts) - owner_counts
    slot_index = jnp.arange(capacity, dtype=jnp.int32)
    picked = starts[None, :] + slot_index[:, None]
    usable = slot_index[:, None] < owner_counts[None, :]
    picked = jnp.where(usable, picked, 0)
    outgoing = jnp.take(moments, picked, axis=1)
    outgoing = jnp.where(usable[None, :, :, None, None], outgoing, 0.0)
    arrived = lax.all_to_all(outgoing, "row", split_axis=2, concat_axis=2, tiled=True)
    arrived = arrived.reshape(tensors, capacity, block_rows, piece_width)
    block_peak = total_of_pieces(jnp.max(jnp.abs(arrived), axis=(2, 3)), "col")
    block_total = over_copies(jnp.sum(arrived * arrived, axis=(2, 3)), "col")
    scales = jnp.maximum(block_peak, 1.0)
    normalized = (arrived / scales[:, :, None, None]).reshape(
        tensors, capacity * block_rows, piece_width
    )
    energy = block_total / (block_rows * full_width)
    return (normalized, scales, energy)


def solution(mesh):
    placed = (P(None, None, "row", "col"), P())
    return jax.shard_map(
        on_device,
        mesh=mesh,
        in_specs=placed,
        out_specs=(P(None, "row", "col"), P(None, "row"), P(None, "row")),
        check_vma=False,
    )
```

profile of v0, /device:TPU:1, one launch (start us, length us, event | category | flops | bytes accessed | tf_op | source)
XLA Modules:
  0.0 226.5 jit_solution(7743040617530875566)
XLA Ops:
  0.6 0.7 copy.16
  1.4 0.1 reduce.3
  1.5 0.7 sub.3
  2.2 0.7 fusion.2
  2.8 0.7 compare_select_fusion
  3.5 0.1 reshape.159
  3.6 8.9 %gather_fusion = f32[256,2,8,768]{3,2,1,0:T(8,128)} fusion(f32[2,128,8,768]{3,2,1,0:T(8,128)} %param.2, s32[1024]{0:T(1024)S(1)} %pad_clamp_fusion), kind=kCustom, calls=%fused_computation | custom fusion | bytes 25166848 | tf_op jit(solution)/shard_map/jit(_take)/gather | solution.py:32
  12.5 9.9 %select_bitcast_fusion = f32[2,16,16,8,768]{4,3,0,2,1:T(8,128)} fusion(f32[16,16,2,8,768]{4,3,2,1,0:T(8,128)} %bitcast.14, pred[16,16]{1,0:T(8,128)(4,1)S(1)} %get-tuple-element.6, pred[16,16]{1,0:T(8,128)(4,1)S(1)} %get-tuple-element.5), kind=kLoop, calls=%fused_computation.2 | loop fusion | flops 6291456 | bytes 25166336 | tf_op jit(solution)/shard_map/jit(_where)/select_n | solution.py:33
  22.4 10.8 %copy.17 = f32[2,16,16,8,768]{4,3,1,0,2:T(8,128)} copy(f32[2,16,16,8,768]{4,3,0,2,1:T(8,128)} %select_bitcast_fusion) | data formatting | bytes 25165824 | tf_op jit(solution)/shard_map/jit(_where)/select_n | solution.py:33
  33.2 147.2 %all_to_all.10 = f32[2,16,16,8,768]{4,3,1,0,2:T(8,128)S(1)} all-to-all(f32[2,16,16,8,768]{4,3,1,0,2:T(8,128)} %copy.17), channel_id=1, replica_groups=mesh['row'=16,'col'=8] {'row'}, dimensions={2} | all-to-all | bytes 25165824 | tf_op jit(solution)/shard_map/all_to_all | solution.py:34
  180.4 0.0 copy-start
  180.4 4.8 %copy-done = f32[2,16,16,8,768]{4,3,1,0,2:T(8,128)} copy-done((f32[2,16,16,8,768]{4,3,1,0,2:T(8,128)}, f32[2,16,16,8,768]{4,3,1,0,2:T(8,128)S(1)}, u32[]{:S(2)}) %copy-start) | copy-done | bytes 12582936
  185.2 1.8 multiply_reduce_fusion
  187.0 13.7 %all-gather.1 = f32[8,2,16]{2,1,0:T(2,128)S(1)} all-gather(f32[1,2,16]{2,1,0:T(2,128)S(1)} %bitcast.17), channel_id=2, replica_groups=mesh['row'=16,'col'=8] {'col'}, dimensions={0}, use_global_device_ids=true | all-gather | bytes 1152 | tf_op jit(solution)/shard_map/all_gather | solution.py:8
  200.8 0.0 copy-start.1
  200.8 0.6 broadcast_in_dim.43
  201.4 3.4 %all-to-all-start.1 = ((f32[8,2,16]{2,1,0:T(2,128)}), f32[8,2,16]{2,1,0:T(2,128)S(1)}, u32[]{:S(2)}, u32[]{:S(2)}) async-start(f32[8,2,16]{2,1,0:T(2,128)} %broadcast_in_dim.43), calls=%async_computation.1 | async-start | bytes 16384 | tf_op jit(solution)/shard_map/all_to_all | solution.py:13
  204.8 0.1 broadcast_bitcast_fusion
  204.8 10.8 %copy.18 = f32[2,16,16,8,768]{4,3,2,1,0:T(8,128)} copy(f32[2,16,16,8,768]{4,3,1,0,2:T(8,128)} %copy-done) | data formatting | bytes 25165824 | tf_op jit(solution)/shard_map/all_to_all | solution.py:34
  215.7 0.0 copy-done.1
  215.7 10.2 %bitcast_divide_fusion = f32[2,2048,768]{2,1,0:T(8,128)} fusion(f32[2,16,16,8,768]{4,3,2,1,0:T(8,128)} %copy.18, f32[2,2048]{1,0:T(2,128)S(1)} %bitcast.15), kind=kLoop, calls=%fused_computation.1 | loop fusion | flops 3145728 | bytes 25182208 | tf_op jit(solution)/shard_map/div | solution.py:39
  225.9 0.0 all-to-all-done.1
  225.9 0.6 broadcast_multiply_fusion
  (6 shorter events, 0.1 us)
Async XLA Ops:
  180.4 4.8 %copy-start = (f32[2,16,16,8,768]{4,3,1,0,2:T(8,128)}, f32[2,16,16,8,768]{4,3,1,0,2:T(8,128)S(1)}, u32[]{:S(2)}) copy-start(f32[2,16,16,8,768]{4,3,1,0,2:T(8,128)S(1)} %all_to_all.10) | copy-start | bytes 37748740
  200.8 14.9 %copy-start.1 = (f32[2,16]{1,0:T(2,128)}, f32[2,16]{1,0:T(2,128)S(1)}, u32[]{:S(2)}) copy-start(f32[2,16]{1,0:T(2,128)S(1)} %broadcast_maximum_fusion) | copy-start | bytes 388
  201.4 24.5 %all-to-all-start.1 = ((f32[8,2,16]{2,1,0:T(2,128)}), f32[8,2,16]{2,1,0:T(2,128)S(1)}, u32[]{:S(2)}, u32[]{:S(2)}) async-start(f32[8,2,16]{2,1,0:T(2,128)} %broadcast_in_dim.43), calls=%async_computation.1 | async-start | bytes 16384 | tf_op jit(solution)/shard_map/all_to_all | solution.py:13
where the time goes:
time: 227 us; the launch traced here: 226 us
  blocking collectives  161 us (71%)
  local copies, waits for them, and re-layouts  36.9 us (16%)
  other arithmetic  24.6 us (11%)
  starting transfers between devices  3.38 us (1%)
    all_to_all x1, blocking collectives, on_device(): lax.all_to_all(outgoing, 'row', split_axis=2, concat_axis=2, tiled=True)  147 us
    all_gather x1, blocking collectives, total_of_pieces(): return lax.all_gather(x, axis).max(0)  13.7 us
    all_to_all x1, local copies, waits for them, and re-layouts, on_device(): lax.all_to_all(outgoing, 'row', split_axis=2, concat_axis=2, tiled=True)  10.8 us
    select_n x1, local copies, waits for them, and re-layouts, on_device(): outgoing = jnp.where(usable[None, :, :, None, None], outgoing, 0.0)  10.8 us
    div x1, other arithmetic, on_device(): arrived / scales[:, :, None, None]  10.2 us
    select_n x1, other arithmetic, on_device(): outgoing = jnp.where(usable[None, :, :, None, None], outgoing, 0.0)  9.88 us
    gather x1, local copies, waits for them, and re-layouts, on_device(): outgoing = jnp.take(moments, picked, axis=1)  8.92 us
    unnamed x6, local copies, waits for them, and re-layouts  4.86 us
  transfers between devices with their start and end apart: 1, of which 0 were waited for; matrix products, arithmetic and copies ran while one was open for 9% of the time, Pallas kernels for 0%

commit v1 on v0

v1 whole, which is shorter than its diff:
```python
import functools

import jax
import jax.numpy as jnp
from jax import lax
from jax.experimental import pallas as pl
from jax.experimental.pallas import tpu as pltpu
from jax.sharding import PartitionSpec as P

CAP = 16


def stats_of(x):
    w = x.shape[-1]
    peak = jnp.abs(x[:, :, :128])
    total = x[:, :, :128] * x[:, :, :128]
    for c in range(128, w, 128):
        piece = x[:, :, c : c + 128]
        peak = jnp.maximum(peak, jnp.abs(piece))
        total = total + piece * piece
    peak = jnp.max(jnp.max(peak, axis=1), axis=1, keepdims=True)
    total = jnp.sum(jnp.sum(total, axis=1), axis=1, keepdims=True)
    return peak, total


def pack_kernel(counts, moments, packed, peak, total, held, sems):
    tensors, blocks = moments.shape[:2]
    groups = packed.shape[0]
    parts = sems.shape[1]
    step = blocks // parts
    copies = [
        [
            pltpu.make_async_copy(
                moments.at[t, pl.ds(p * step, step)],
                held.at[t, pl.ds(p * step, step)],
                sems.at[t, p],
            )
            for p in range(parts)
        ]
        for t in range(tensors)
    ]
    for t in range(tensors):
        for p in range(parts):
            copies[t][p].start()
    for t in range(tensors):
        for p in range(parts):
            copies[t][p].wait()

            def take_stats(i, _):
                at = pl.multiple_of(p * step + i * 8, 8)
                m, s = stats_of(held[t, pl.ds(at, 8)])
                peak[t, pl.ds(at, 8)] = m
                total[t, pl.ds(at, 8)] = s
                return 0

            lax.fori_loop(0, step // 8, take_stats, 0)

    def group(g, start):
        def slot(j, _):
            for t in range(tensors):
                packed[g, t, j] = held[t, start + j]
            return 0

        lax.fori_loop(0, counts[g], slot, 0)
        return start + counts[g]

    lax.fori_loop(0, groups, group, jnp.int32(0))


def place_kernel(info, inverse, arrived, out):
    t, j = pl.program_id(0), pl.program_id(1)
    sources, sub = arrived.shape[0], arrived.shape[3]

    @pl.when(j < info[0])
    def _():
        scale = inverse[t, j]
        for s in range(sources):
            out[0, s * sub : (s + 1) * sub, :] = arrived[s, t, j] * scale

    @pl.when(j >= info[0])
    def _():
        out[...] = jnp.zeros_like(out)


def on_device(moments, owner_counts):
    groups = lax.axis_size("row")
    splits = lax.axis_size("col")
    tensors, blocks, sub, width = moments.shape
    block_rows = sub * groups
    full_width = width * splits
    me = lax.axis_index("row")
    smem = pl.BlockSpec(memory_space=pltpu.SMEM)
    vmem = pl.BlockSpec(memory_space=pltpu.VMEM)
    parts = 4

    packed, peak, total = pl.pallas_call(
        pack_kernel,
        out_shape=(
            jax.ShapeDtypeStruct((groups, tensors, CAP, sub, width), jnp.float32),
            jax.ShapeDtypeStruct((tensors, blocks, 1), jnp.float32),
            jax.ShapeDtypeStruct((tensors, blocks, 1), jnp.float32),
        ),
        in_specs=[smem, pl.BlockSpec(memory_space=pl.ANY)],
        out_specs=(vmem, vmem, vmem),
        scratch_shapes=[
            pltpu.VMEM((tensors, blocks, sub, width), jnp.float32),
            pltpu.SemaphoreType.DMA((tensors, parts)),
        ],
        name="pack",
    )(owner_counts, moments)

    starts = jnp.cumsum(owner_counts) - owner_counts
    both = jnp.stack([peak[..., 0], total[..., 0]])
    both = lax.all_gather(both, "row")
    mine = jnp.minimum(starts[me] + jnp.arange(CAP), blocks - 1)
    both = jnp.stack([both[:, 0].max(0), both[:, 1].sum(0)])
    both = jnp.take(both, mine, axis=2)
    both = lax.all_gather(both, "col")
    used = jnp.arange(CAP) < owner_counts[me]
    block_peak = jnp.where(used, both[:, 0].max(0), 0.0)
    block_total = jnp.where(used, both[:, 1].sum(0), 0.0)
    scales = jnp.maximum(block_peak, 1.0)
    energy = block_total / (block_rows * full_width)

    arrived = lax.all_to_all(packed, "row", split_axis=0, concat_axis=0, tiled=True)
    normalized = pl.pallas_call(
        place_kernel,
        grid=(tensors, CAP),
        out_shape=jax.ShapeDtypeStruct((tensors, CAP * block_rows, width), jnp.float32),
        in_specs=[smem, smem, vmem],
        out_specs=pl.BlockSpec((1, block_rows, width), lambda t, j: (t, j, 0)),
        name="place",
    )(owner_counts[me][None], 1.0 / scales, arrived)
    return normalized, scales, energy


def solution(mesh):
    return jax.shard_map(
        on_device,
        mesh=mesh,
        in_specs=(P(None, None, "row", "col"), P()),
        out_specs=(P(None, "row", "col"), P(None, "row"), P(None, "row")),
        check_vma=False,
    )
```

time: 227 us -> 257 us (1.13)
  blocking collectives: 161 us -> 214 us
  local copies, waits for them, and re-layouts: 36.9 us -> 2.17 us
  Pallas kernels: 0 us -> 29.4 us
  other arithmetic: 24.6 us -> 3.01 us
  starting transfers between devices: 3.38 us -> 7.76 us
    all_gather x1 -> x2, blocking collectives: 13.7 us -> 214 us  [the longest x1 196 us: on_device(): both = lax.all_gather(both, 'row')]
    all_to_all x1 -> x0, blocking collectives: 147 us -> none  [on_device(): lax.all_to_all(outgoing, 'row', split_axis=2, concat_axis=2, tiled=True)]
    pallas_call x0 -> x2, Pallas kernels: none -> 29.4 us  [the longest x1 18.1 us: on_device(): pl.pallas_call(place_kernel, grid=(tensors, CAP), out_shape=jax.ShapeDtyp...]
    select_n x2 -> x0, local copies, waits for them, and re-layouts: 10.9 us -> none  [the longest x1 10.8 us: on_device(): outgoing = jnp.where(usable[None, :, :, None, None], outgoing, 0.0)]
    all_to_all x1 -> x0, local copies, waits for them, and re-layouts: 10.8 us -> none  [on_device(): lax.all_to_all(outgoing, 'row', split_axis=2, concat_axis=2, tiled=True)]
    div x2 -> x1, other arithmetic: 10.8 us -> 0.59 us  [on_device(): 1.0 / scales]
    select_n x2, other arithmetic: 10.5 us -> 0.66 us  [on_device(): both = jnp.take(both, mine, axis=2)]
    gather x1 -> x2, local copies, waits for them, and re-layouts: 8.92 us -> 0.68 us  [on_device(): both = jnp.take(both, mine, axis=2)]
  transfers between devices with their start and end apart: 1 -> 1, of which waited for: 0 -> 0; matrix products, arithmetic and copies ran while one was open for 9% -> 2% of each run, Pallas kernels for 0% -> 0%
where the time goes in v1:
time: 257 us
  blocking collectives  214 us (83%)
  Pallas kernels  29.4 us (11%)
  starting transfers between devices  7.76 us (3%)
  other arithmetic  3.01 us (1%)
    all_gather x1, blocking collectives, on_device(): both = lax.all_gather(both, 'row')  196 us
    pallas_call x1, Pallas kernels, on_device(): pl.pallas_call(place_kernel, grid=(tensors, CAP), out_shape=jax.ShapeDtyp...  18.1 us
    all_gather x1, blocking collectives, on_device(): both = lax.all_gather(both, 'col')  18.1 us
    pallas_call x1, Pallas kernels, on_device(): pl.pallas_call(pack_kernel, out_shape=(jax.ShapeDtypeStruct((groups, tens...  11.3 us
    all_to_all x1, starting transfers between devices, on_device(): lax.all_to_all(packed, 'row', split_axis=0, concat_axis=0, tiled=True)  7.76 us
  transfers between devices with their start and end apart: 1, of which 0 were waited for; matrix products, arithmetic and copies ran while one was open for 2% of the time, Pallas kernels for 0%

profile of v1, /device:TPU:1, one launch (start us, length us, event | category | flops | bytes accessed | tf_op | source)
XLA Modules:
  0.0 256.8 jit_solution(10901743034622510161)
XLA Ops:
  0.6 11.3 %pack.1 = (f32[16,2,16,8,768]{4,3,2,1,0:T(8,128)}, f32[2,128,1]{2,1,0:T(8,128)}, f32[2,128,1]{2,1,0:T(8,128)}) custom-call(s32[16]{0:T(128)} %counts.1, f32[2,128,8,768]{3,2,1,0:T(8,128)} %moments.1), custom_call_target="tpu_custom_call" | custom-call | tf_op jit(solution)/shard_map/pack/pallas_call | solution.py:96
  11.9 0.0 copy-start.1
  11.9 0.0 copy-start
  12.0 0.0 copy-start.2
  12.0 7.8 %all-to-all-start = ((f32[16,2,16,8,768]{4,3,2,1,0:T(8,128)}), f32[16,2,16,8,768]{4,3,2,1,0:T(8,128)}, u32[]{:S(2)}, u32[]{:S(2)}) async-start(f32[16,2,16,8,768]{4,3,2,1,0:T(8,128)} %get-tuple-element.8), calls=%async_computation | async-start | bytes 25165824 | tf_op jit(solution)/shard_map/all_to_all | solution.py:125
  19.7 0.0 copy-done.1
  19.8 0.1 reduce.6
  19.9 0.0 copy-done
  19.9 0.1 reduce.5
  20.0 195.6 %all-gather = f32[32,2,128]{2,1,0:T(2,128)S(1)} all-gather(f32[2,2,128]{2,1,0:T(2,128)S(1)} %pad_maximum_fusion), channel_id=2, replica_groups=mesh['row'=16,'col'=8] {'row'}, dimensions={0}, use_global_device_ids=true | all-gather | bytes 34816 | tf_op jit(solution)/shard_map/all_gather | solution.py:114
  215.7 0.2 copy.9
  215.8 0.0 copy-done.2
  215.8 0.1 copy.8
  216.0 0.1 reduce.4
  216.1 0.7 dynamic_slice.7.info
  216.7 0.6 dynamic_slice.8
  217.3 0.7 fusion
  218.0 0.6 gather_fusion
  218.6 0.1 copy.10
  218.7 0.7 compare_and_fusion
  219.4 18.1 %all_gather.12 = f32[8,2,2,16]{3,2,1,0:T(2,128)S(1)} all-gather(f32[1,2,2,16]{3,2,1,0:T(2,128)S(1)} %bitcast_select_fusion), channel_id=1, replica_groups=mesh['row'=16,'col'=8] {'col'}, dimensions={0}, use_global_device_ids=true | all-gather | bytes 2304 | tf_op jit(solution)/shard_map/all_gather | solution.py:118
  237.4 0.7 iota_compare_fusion
  238.2 0.6 broadcast_divide_fusion
  238.7 0.0 all-to-all-done.arrived
  238.7 18.1 %place.1 = f32[2,2048,768]{2,1,0:T(8,128)} custom-call(s32[1]{0:T(128)} %dynamic_slice.7.info, f32[2,16]{1,0:T(2,128)} %get-tuple-element.13.inverse, f32[16,2,16,8,768]{4,3,2,1,0:T(8,128)} %all-to-all-done.arrived), custom_call_target="tpu_custom_call" | custom-call | tf_op jit(solution)/shard_map/place/pallas_call | solution.py:126
  (8 shorter events, 0.1 us)
Async XLA Ops:
  11.9 7.8 %copy-start.1 = (f32[2,128,1]{2,1,0:T(8,128)S(1)}, f32[2,128,1]{2,1,0:T(8,128)}, u32[]{:S(2)}) copy-start(f32[2,128,1]{2,1,0:T(8,128)} %get-tuple-element.7) | copy-start | bytes 3076
  11.9 7.9 %copy-start = (f32[2,128,1]{2,1,0:T(8,128)S(1)}, f32[2,128,1]{2,1,0:T(8,128)}, u32[]{:S(2)}) copy-start(f32[2,128,1]{2,1,0:T(8,128)} %get-tuple-element.6) | copy-start | bytes 3076
  12.0 203.9 %copy-start.2 = (s32[16]{0:T(128)S(1)}, s32[16]{0:T(128)}, u32[]{:S(2)}) copy-start(s32[16]{0:T(128)} %counts.1) | copy-start | bytes 196
  12.0 226.8 %all-to-all-start = ((f32[16,2,16,8,768]{4,3,2,1,0:T(8,128)}), f32[16,2,16,8,768]{4,3,2,1,0:T(8,128)}, u32[]{:S(2)}, u32[]{:S(2)}) async-start(f32[16,2,16,8,768]{4,3,2,1,0:T(8,128)} %get-tuple-element.8), calls=%async_computation | async-start | bytes 25165824 | tf_op jit(solution)/shard_map/all_to_all | solution.py:125
